TPU v7x, 128 devices: a whole 4x4x4 slice. The times are simulated.
128 devices in a mesh: seq: 8 (over z, core), head: 16 (over x, y).
Axes of the slice: x: 4, y: 4, z: 4, core: 2. Of those that a mesh axis runs over, the one named last changes fastest.
Arguments:
- lengths: int32 [16], replicated, may hold values from 128 to 8192, as said below
- page_owner: int32 [1536], replicated, may hold values from 0 to 16, as said below
- page_index: int32 [1536], replicated, may hold values from 0 to 127, as said below
- page_dest: int32 [1536], replicated, may hold values from 0 to 1535, as said below
- src_cache: bfloat16 [1536, 8, 64, 256], P(('seq', 'head')), may hold values from -8 to 8
- queries: bfloat16 [2, 16, 4096], replicated, may hold values from -8 to 8
- new_kv: bfloat16 [2, 16, 8, 256], replicated, may hold values from -6 to 6
- hidden_in: bfloat16 [2, 16, 4096], P(None, None, ('seq', 'head')), may hold values from -60 to 60
- out_weight: bfloat16 [4096, 4096], P(None, ('seq', 'head')), may hold values from -1.5 to 1.5
- norm_gain: bfloat16 [4096], P(('seq', 'head')), may hold values from 0.099609375 to 1.8984375
- router: bfloat16 [4096, 8], P(('seq', 'head')), may hold values from -0.09375 to 0.09375
- routes: int32 [2, 16, 2], replicated, may hold values from 0 to 7, all different within a row
- w_gate: bfloat16 [8, 4096, 8192], P('seq', None, 'head'), may hold values from -0.09375 to 0.09375
- w_up: bfloat16 [8, 4096, 8192], P('seq', None, 'head'), may hold values from -0.09375 to 0.09375
- w_down: bfloat16 [8, 8192, 4096], P('seq', 'head'), may hold values from -0.0625 to 0.0625
Outputs:
- page_pool: bfloat16 [16, 768, 64, 256], P('head', 'seq')
- mixed: bfloat16 [2, 16, 4096], P(None, None, ('seq', 'head'))
Inputs may be any that keep to these rules, and one draw needn't show every extreme that they name: Each length is at least 128; one equals 8192; the requests' pages, lengths[r] / 64 rounded up for request r, fit into the 1536 pages. `page_owner`: request r owns exactly lengths[r] / 64 rounded up source pages; the other pages carry 16. `page_index`: the pages of request r carry 0 to their count minus 1, each once; pages without request carry 0. `page_dest`: A permutation. Slot g belongs to destination group ((g % 768) // 96) * 2 + g // 768. Of the 12 pages that one device holds (pages i * 12 to (i + 1) * 12 - 1), at most 1 go to one group, and every draw has a device that sends exactly 1 to some group.
All inputs are finite; a program needn't handle non-finite values.
Results may differ from a plain program's by a relative error of at most 0.009.
Values may be sent and summed in bfloat16 or wider, within the bound.
A program may use at most 128 MiB of HBM per device.

v0:
```python
import jax
import jax.numpy as jnp
from jax import lax
from jax.sharding import Mesh
from jax.sharding import PartitionSpec as P

D = 4096
HQ = 32
KVH = 8
HD = 128
TOPK = 2
PAGE = 64
REQS = 16
SEQ = ("seq_0", "seq_1")
HEAD = ("head_0", "head_1")
SEQ_HEAD = ("seq_0", "seq_1", "head_0", "head_1")
NEG_FILL = -1e30
EPSILON = 1e-05
HIGHEST = lax.Precision.HIGHEST


def joined_all(array, axes, combine):
    for axis in axes:
        pieces = jax.tree.map(lambda part: lax.all_gather(part, axis), array)
        array = jax.tree.map(lambda part: part[0], pieces)
        for k in range(1, lax.axis_size(axis)):
            array = combine(array, jax.tree.map(lambda part: part[k], pieces))
    return array


def over_axes(array, axes):
    for axis in axes:
        array = lax.psum(array, axis)
    return array


def in_blocks(array, dim, peers):
    lengths = array.shape
    blocks = array.reshape(*lengths[:dim], peers, lengths[dim] // peers, *lengths[dim + 1 :])
    return jnp.moveaxis(blocks, dim, 0)


def cut_rows(length, count):
    unit = 8 if length >= 8 * count else 1
    return [length // unit * k // count * unit for k in range(1, count)]


def own_block(blocks, axes, sequence):
    lengths = [lax.axis_size(a) for a in axes]
    blocks = blocks.reshape(*lengths, *blocks.shape[1:])
    blocks = blocks.transpose(*sequence, *range(len(axes), blocks.ndim))
    blocks = blocks.reshape(-1, *blocks.shape[len(axes) :])
    for k in sequence:
        blocks = lax.psum_scatter(blocks, axes[k], scatter_dimension=0, tiled=True)
    return blocks[0]


def sum_all_axes_2(array, axes, dim):
    blocks = in_blocks(array, dim, lax.axis_size(axes))
    widest = max(range(1, max(2, blocks.ndim - 1)), key=lambda d: blocks.shape[d])
    count, gathered = (len(axes), [])
    for initial, share in enumerate(
        jnp.split(blocks, cut_rows(blocks.shape[widest], count), axis=widest)
    ):
        if share.size:
            sequence = [(initial + k) % count for k in range(count)]
            gathered.append(own_block(share, axes, sequence))
    return jnp.concatenate(gathered, axis=widest - 1)


def gate_mix(logits, picked):
    expert_ids = jnp.arange(logits.shape[1], dtype=jnp.int32)[None, :]
    first_hit = picked[:, 0:1] == expert_ids
    second_hit = picked[:, 1:2] == expert_ids
    first_logit = jnp.sum(jnp.where(first_hit, logits, 0.0), axis=1)
    second_logit = jnp.sum(jnp.where(second_hit, logits, 0.0), axis=1)
    leading = 1.0 / (1.0 + jnp.exp(second_logit - first_logit))
    trailing = 1.0 / (1.0 + jnp.exp(first_logit - second_logit))
    return jnp.where(first_hit, leading[:, None], 0.0) + jnp.where(
        second_hit, trailing[:, None], 0.0
    )


def combine(earlier, later):
    first_top, first_sum, first_acc = earlier
    second_top, second_sum, second_acc = later
    joint_top = jnp.maximum(first_top, second_top)
    first_factor = jnp.exp(first_top - joint_top)
    second_factor = jnp.exp(second_top - joint_top)
    return (
        joint_top,
        first_sum * first_factor + second_sum * second_factor,
        first_acc * first_factor[..., None] + second_acc * second_factor[..., None],
    )


def slot_plan(page_dest, pages_dev, slot_count, slots_dev, replicas, groups):
    part_index = page_dest // slot_count
    within = page_dest % slot_count
    target = within // slots_dev * replicas + part_index
    position = within % slots_dev
    per_device = target.reshape(-1, pages_dev)
    onehot = (per_device[:, :, None] == jnp.arange(groups, dtype=jnp.int32)[None, None, :]).astype(
        jnp.int32
    )
    before = jnp.cumsum(onehot, axis=1) - onehot
    ranking = jnp.sum(before * onehot, axis=2).reshape(-1)
    return (target, position, ranking)


def partial_attention(page_block, owners, page_pos, lengths, grouped, score_scale):
    head_dim = grouped.shape[-1]
    page_len = page_block.shape[2]
    requests = grouped.shape[1]
    clipped = jnp.minimum(owners, requests - 1)
    length_cap = jnp.take(lengths, clipped)
    offsets = page_pos[:, None] * page_len + jnp.arange(page_len, dtype=jnp.int32)[None, :]
    is_live = (owners < requests)[:, None] & (offsets < length_cap[:, None])
    live_mask = is_live[None, :, None, None, :]
    asked_rows = jnp.take(grouped, clipped, axis=1)
    scores = (
        jnp.einsum(
            "spkgd,pktd->spkgt",
            asked_rows,
            page_block[..., :head_dim],
            preferred_element_type=jnp.float32,
        )
        * score_scale
    )
    scores = jnp.where(live_mask, scores, NEG_FILL)
    members = owners[:, None] == jnp.arange(requests, dtype=jnp.int32)[None, :]
    page_top = jnp.max(scores, axis=4)
    row_top = jnp.max(
        jnp.where(members[None, :, :, None, None], page_top[:, :, None], NEG_FILL), axis=1
    )
    weights = jnp.where(
        live_mask, jnp.exp(scores - jnp.take(row_top, clipped, axis=1)[..., None]), 0.0
    )
    member_mask = members.astype(jnp.float32)
    totals = jnp.einsum("pr,spkg->srkg", member_mask, jnp.sum(weights, axis=4), precision=HIGHEST)
    page_out = jnp.einsum(
        "spkgt,pktd->spkgd",
        weights.astype(jnp.bfloat16),
        page_block[..., head_dim:],
        preferred_element_type=jnp.float32,
    )
    weighted = jnp.einsum("pr,spkgd->srkgd", member_mask, page_out, precision=HIGHEST)
    return (row_top, totals, weighted)


def body(
    lengths,
    page_owner,
    page_index,
    page_dest,
    src_cache,
    queries,
    new_kv,
    hidden_in,
    out_weight,
    norm_gain,
    router,
    routes,
    w_gate,
    w_up,
    w_down,
):
    seq_count = lax.axis_size(SEQ)
    head_count = lax.axis_size(HEAD)
    device_count = seq_count * head_count
    seq_pos = lax.axis_index(SEQ)
    head_pos = lax.axis_index(HEAD)
    pages_dev = src_cache.shape[0]
    page_total = page_dest.shape[0]
    replicas = head_count // KVH
    groups = seq_count * replicas
    slot_count = page_total // replicas
    slots_dev = pages_dev * KVH
    capacity = (slots_dev + device_count - 1) // device_count
    group_size = HQ // KVH
    step_count = queries.shape[0]
    row_count = step_count * REQS
    source = seq_pos * head_count + head_pos
    target, position, ranking = slot_plan(
        page_dest, pages_dev, slot_count, slots_dev, replicas, groups
    )
    local_target = lax.dynamic_slice_in_dim(target, source * pages_dev, pages_dev)
    local_rank = lax.dynamic_slice_in_dim(ranking, source * pages_dev, pages_dev)
    wanted = jnp.arange(groups * capacity, dtype=jnp.int32)
    matches = (local_target[None, :] == (wanted // capacity)[:, None]) & (
        local_rank[None, :] == (wanted % capacity)[:, None]
    )
    picked_page = jnp.sum(
        jnp.where(matches, jnp.arange(pages_dev, dtype=jnp.int32)[None, :], 0), axis=1
    )
    filled = jnp.any(matches, axis=1)
    packed = jnp.where(
        filled[:, None, None, None],
        jnp.take(src_cache, picked_page, axis=0),
        jnp.zeros((), jnp.bfloat16),
    )
    packed = packed.reshape(seq_count, replicas, capacity, KVH, PAGE, 2 * HD).transpose(
        0, 3, 1, 2, 4, 5
    )
    arrived = lax.all_to_all(
        packed.reshape(device_count, capacity, PAGE, 2 * HD),
        SEQ_HEAD,
        split_axis=0,
        concat_axis=0,
        tiled=True,
    )
    arrived = arrived.reshape(device_count * capacity, PAGE, 2 * HD)
    my_group = seq_pos * replicas + head_pos % replicas
    slot_ids = jnp.arange(slots_dev, dtype=jnp.int32)
    holders = (target[None, :] == my_group) & (position[None, :] == slot_ids[:, None])
    flat_index = jnp.arange(page_total, dtype=jnp.int32) // pages_dev * capacity + ranking
    chosen = jnp.sum(jnp.where(holders, flat_index[None, :], 0), axis=1)
    page_pool = jnp.take(arrived, chosen, axis=0)
    grouped = queries.reshape(step_count, REQS, KVH, group_size, HD)
    score_scale = HD ** (-0.5)
    kv_head = head_pos // replicas
    owners = jnp.sum(jnp.where(holders, page_owner[None, :], 0), axis=1)
    places = jnp.sum(jnp.where(holders, page_index[None, :], 0), axis=1)
    own_queries = lax.dynamic_slice_in_dim(grouped, kv_head, 1, axis=2)
    row_top, totals, weighted = partial_attention(
        page_pool[:, None], owners, places, lengths, own_queries, score_scale
    )
    owned_head = (jnp.arange(KVH, dtype=jnp.int32) == kv_head)[None, None, :, None]
    row_top = jnp.where(owned_head, row_top, NEG_FILL)
    totals = jnp.where(owned_head, totals, 0.0)
    weighted = jnp.where(owned_head[..., None], weighted, 0.0)
    row_top, totals, weighted = joined_all(
        (
            row_top.reshape(step_count, REQS, HQ),
            totals.reshape(step_count, REQS, HQ),
            weighted.reshape(step_count, REQS, HQ, HD),
        ),
        SEQ_HEAD,
        combine,
    )
    fresh_scores = (
        jnp.einsum(
            "srkgd,urkd->srkgu", grouped, new_kv[..., :HD], preferred_element_type=jnp.float32
        )
        * score_scale
    )
    causal = (jnp.arange(step_count)[:, None] >= jnp.arange(step_count)[None, :])[:, None, None, :]
    fresh_scores = jnp.where(
        causal, fresh_scores.reshape(step_count, REQS, HQ, step_count), NEG_FILL
    )
    joint_top = jnp.maximum(row_top, jnp.max(fresh_scores, axis=3))
    factor = jnp.exp(row_top - joint_top)
    fresh_weights = jnp.where(causal, jnp.exp(fresh_scores - joint_top[..., None]), 0.0)
    totals = totals * factor + jnp.sum(fresh_weights, axis=3)
    fresh_rounded = fresh_weights.reshape(step_count, REQS, KVH, group_size, step_count).astype(
        jnp.bfloat16
    )
    fresh_out = jnp.einsum(
        "srkgu,urkd->srkgd", fresh_rounded, new_kv[..., HD:], preferred_element_type=jnp.float32
    )
    weighted = weighted * factor[..., None] + fresh_out.reshape(step_count, REQS, HQ, HD)
    attended = (weighted / totals[..., None]).reshape(row_count, HQ * HD).astype(jnp.bfloat16)
    attn_out = jnp.dot(attended, out_weight, preferred_element_type=jnp.float32)
    middle = hidden_in.reshape(row_count, -1).astype(jnp.float32) + attn_out
    gain_row = norm_gain.astype(jnp.float32)[None, :]
    squares, routed = (
        over_axes(jnp.sum(middle * middle, axis=1), SEQ_HEAD),
        over_axes(
            jnp.dot(middle * gain_row, router.astype(jnp.float32), precision=HIGHEST), SEQ_HEAD
        ),
    )
    inverse_rms = lax.rsqrt(squares / D + EPSILON)
    logits = routed * inverse_rms[:, None]
    normed = (middle * inverse_rms[:, None] * gain_row).astype(jnp.bfloat16)
    features = lax.all_gather(normed, SEQ_HEAD, axis=1, tiled=True)
    mixture = gate_mix(logits, routes.reshape(row_count, TOPK))
    local_experts = w_gate.shape[0]
    local_mix = lax.dynamic_slice_in_dim(mixture, seq_pos * local_experts, local_experts, axis=1)
    gate_act = jnp.einsum("rd,edf->erf", features, w_gate, preferred_element_type=jnp.float32)
    upward = jnp.einsum("rd,edf->erf", features, w_up, preferred_element_type=jnp.float32)
    inner_act = (jax.nn.silu(gate_act) * upward).astype(jnp.bfloat16)
    produced = jnp.einsum("erf,efd->erd", inner_act, w_down, preferred_element_type=jnp.float32)
    moe_out = sum_all_axes_2(jnp.sum(local_mix.T[:, :, None] * produced, axis=0).T, SEQ_HEAD, 0)
    mixed = (middle + moe_out.T).astype(jnp.bfloat16).reshape(step_count, REQS, -1)
    return (page_pool[None], mixed)


def solution(mesh):
    split = Mesh(mesh.devices.reshape(4, 2, 4, 4), ("seq_0", "seq_1", "head_0", "head_1"))
    in_specs = (
        P(),
        P(),
        P(),
        P(),
        P(SEQ_HEAD, None, None, None),
        P(),
        P(),
        P(None, None, SEQ_HEAD),
        P(None, SEQ_HEAD),
        P(SEQ_HEAD),
        P(SEQ_HEAD, None),
        P(),
        P(SEQ, None, HEAD),
        P(SEQ, None, HEAD),
        P(SEQ, HEAD, None),
    )
    out_specs = (P(HEAD, SEQ, None, None), P(None, None, SEQ_HEAD))
    return jax.shard_map(body, mesh=split, in_specs=in_specs, out_specs=out_specs, check_vma=False)
```

profile of v0, /device:TPU:0, one launch (start us, length us, event | category | flops | bytes accessed | tf_op | source)
XLA Modules:
  0.0 609.9 jit_solution(12945465828086669318)
XLA Ops:
  7.2 0.9 broadcast_compare_fusion
  9.1 2.7 gather_fusion
  11.9 2.7 select_bitcast_fusion
  14.6 2.3 copy.230
  16.9 11.7 %all-to-all-start = ((bf16[128,1,64,256]{3,2,1,0:T(8,128)(2,1)}), bf16[128,1,64,256]{3,2,1,0:T(8,128)(2,1)}, u32[]{:S(2)}, u32[]{:S(2)}) async-start(bf16[128,1,64,256]{3,2,1,0:T(8,128)(2,1)} %bitcast.483), calls=%async_computation | async-start | bytes 8388608 | tf_op jit(solution)/shard_map/all_to_all | solution.py:205
  29.6 1.5 gather_fusion.2
  31.1 0.7 fusion.149
  31.8 9.8 %fusion.130 = (s32[96]{0:T(128)S(1)}, s32[96]{0:T(128)S(1)}) fusion(s32[]{:T(128)} %bitcast.17, s32[]{:T(128)} %bitcast.18, s32[]{:T(128)} %bitcast.19, s32[]{:T(128)} %bitcast.20, s32[]{:T(128)} %bitcast.21, s32[]{:T(128)} %bitcast.22, s32[]{:T(128)} %bitcast.23, s32[]{:T(128)} %bitcast.24, s32[]{:T(128)} %bitcast.25, s32[]{:T(128)} %bitcast.26, ...), kind=kLoop, calls=%fused_computation.273 | loop fusion | flops 4032 | bytes 1600 | tf_op jit(solution)/shard_map/jit(_take)/select_n | solution.py:116
  41.7 38.0 %all-to-all-done = bf16[128,1,64,256]{3,2,1,0:T(8,128)(2,1)} async-done(((bf16[128,1,64,256]{3,2,1,0:T(8,128)(2,1)}), bf16[128,1,64,256]{3,2,1,0:T(8,128)(2,1)}, u32[]{:S(2)}, u32[]{:S(2)}) %all-to-all-start) | async-done | bytes 4194336 | tf_op jit(solution)/shard_map/all_to_all | solution.py:205
  79.7 3.0 gather_fusion.1
  83.0 1.3 copy-done.2
  84.3 1.7 copy-done.4
  86.0 1.2 fusion.151
  87.5 0.7 gather_fusion.3
  88.4 2.0 fusion.8
  90.8 0.9 broadcast_select_fusion
  92.8 12.2 %all_gather.49 = f32[4,2,16,32]{3,2,1,0:T(8,128)S(1)} all-gather(f32[1,2,16,32]{3,2,1,0:T(8,128)S(1)} %copy.236), channel_id=1, replica_groups=mesh['seq_0'=4,'seq_1'=2,'head_0'=4,'head_1'=4] {'seq_0'}, dimensions={0}, use_global_device_ids=true | all-gather | bytes 20480 | tf_op jit(solution)/shard_map/all_gather | solution.py:24
  105.0 14.8 %all-gather.5.cloned.1.call-done = f32[4,2,16,32,128]{4,3,2,1,0:T(8,128)} async-done(((f32[1,2,16,32,128]{4,3,2,1,0:T(8,128)}), f32[4,2,16,32,128]{4,3,2,1,0:T(8,128)}) %all-gather.5.cloned.1.call-update) | async-done | bytes 2097168 | tf_op jit(solution)/shard_map/all_gather | solution.py:24
  119.8 2.9 fusion.45
  122.8 12.0 %all_gather.56 = f32[4,2,16,32]{3,2,1,0:T(8,128)S(1)} all-gather(f32[1,2,16,32]{3,2,1,0:T(8,128)S(1)} %copy.255), channel_id=1, replica_groups=mesh['seq_0'=4,'seq_1'=2,'head_0'=4,'head_1'=4] {'seq_0'}, dimensions={0}, use_global_device_ids=true | all-gather | bytes 20480 | tf_op jit(solution)/shard_map/all_gather | solution.py:24
  134.9 1.8 all_gather.51
  136.7 2.3 fusion.44
  139.2 1.8 all_gather.57
  141.0 12.1 %all_gather.53 = f32[4,2,16,32]{3,2,1,0:T(8,128)S(1)} all-gather(f32[1,2,16,32]{3,2,1,0:T(8,128)S(1)} %get-tuple-element.32), channel_id=1, replica_groups=mesh['seq_0'=4,'seq_1'=2,'head_0'=4,'head_1'=4] {'head_0'}, dimensions={0}, use_global_device_ids=true | all-gather | bytes 20480 | tf_op jit(solution)/shard_map/all_gather | solution.py:24
  153.1 16.3 %all-gather.9.cloned.1.call-done = f32[4,2,16,32,128]{4,3,2,1,0:T(8,128)} async-done(((f32[1,2,16,32,128]{4,3,2,1,0:T(8,128)}), f32[4,2,16,32,128]{4,3,2,1,0:T(8,128)}) %all-gather.9.cloned.1.call-update) | async-done | bytes 2097168 | tf_op jit(solution)/shard_map/all_gather | solution.py:24
  169.5 2.9 fusion.39
  172.5 2.4 fusion.152
  175.3 11.9 %all_gather.58 = f32[4,2,16,32]{3,2,1,0:T(8,128)S(1)} all-gather(f32[1,2,16,32]{3,2,1,0:T(8,128)S(1)} %get-tuple-element.31), channel_id=1, replica_groups=mesh['seq_0'=4,'seq_1'=2,'head_0'=4,'head_1'=4] {'head_0'}, dimensions={0}, use_global_device_ids=true | all-gather | bytes 20480 | tf_op jit(solution)/shard_map/all_gather | solution.py:24
  187.1 13.0 %all_gather.55 = f32[4,2,16,32]{3,2,1,0:T(8,128)S(1)} all-gather(f32[1,2,16,32]{3,2,1,0:T(8,128)S(1)} %get-tuple-element.30), channel_id=1, replica_groups=mesh['seq_0'=4,'seq_1'=2,'head_0'=4,'head_1'=4] {'head_1'}, dimensions={0}, use_global_device_ids=true | all-gather | bytes 20480 | tf_op jit(solution)/shard_map/all_gather | solution.py:24
  201.5 11.9 %all_gather.59 = f32[4,2,16,32]{3,2,1,0:T(8,128)S(1)} all-gather(f32[1,2,16,32]{3,2,1,0:T(8,128)S(1)} %get-tuple-element.29), channel_id=1, replica_groups=mesh['seq_0'=4,'seq_1'=2,'head_0'=4,'head_1'=4] {'head_1'}, dimensions={0}, use_global_device_ids=true | all-gather | bytes 20480 | tf_op jit(solution)/shard_map/all_gather | solution.py:24
  215.1 1.8 fusion.145
  218.5 3.6 multiply_reduce_fusion
  222.3 10.7 %all-reduce.6 = (f32[32]{0:T(128)S(1)}, f32[32,8]{0,1:T(8,128)S(1)}) all-reduce(f32[32]{0:T(128)S(1)} %get-tuple-element.95, f32[32,8]{0,1:T(8,128)S(1)} %fusion.112), channel_id=1, replica_groups=mesh['seq_0'=4,'seq_1'=2,'head_0'=4,'head_1'=4] {'seq_0'}, use_global_device_ids=true, to_apply=%region_17.18 | all-reduce | flops 288 | bytes 2304 | tf_op jit(solution)/shard_map/psum | solution.py:33
  233.0 2.5 all-reduce.7
  235.5 8.7 %all-reduce.5 = (f32[32]{0:T(128)S(1)}, f32[32,8]{0,1:T(8,128)S(1)}) all-reduce(f32[32]{0:T(128)S(1)} %get-tuple-element.15, f32[32,8]{0,1:T(8,128)S(1)} %get-tuple-element.16), channel_id=1, replica_groups=mesh['seq_0'=4,'seq_1'=2,'head_0'=4,'head_1'=4] {'head_0'}, use_global_device_ids=true, to_apply=%region_19.20 | all-reduce | flops 288 | bytes 2304 | tf_op jit(solution)/shard_map/psum | solution.py:33
  244.3 10.3 %all-reduce.4 = (f32[32]{0:T(128)S(1)}, f32[32,8]{0,1:T(8,128)S(1)}) all-reduce(f32[32]{0:T(128)S(1)} %get-tuple-element.11, f32[32,8]{0,1:T(8,128)S(1)} %get-tuple-element.12), channel_id=1, replica_groups=mesh['seq_0'=4,'seq_1'=2,'head_0'=4,'head_1'=4] {'head_1'}, use_global_device_ids=true, to_apply=%region_20.21 | all-reduce | flops 288 | bytes 2304 | tf_op jit(solution)/shard_map/psum | solution.py:33
  254.6 60.0 %all_gather.60 = bf16[32,4096]{0,1:T(8,128)(2,1)S(1)} all-gather(bf16[32,32]{0,1:T(8,128)(2,1)S(1)} %multiply_convert_fusion), channel_id=1, replica_groups=mesh['seq_0'=4,'seq_1'=2,'head_0'=4,'head_1'=4] {'seq_0','seq_1','head_0..., dimensions={1}, use_global_device_ids=true | all-gather | bytes 264192 | tf_op jit(solution)/shard_map/all_gather | solution.py:275
  314.7 3.0 fusion.14
  317.7 5.1 fusion
  322.8 0.7 reshape.805
  323.5 4.9 fusion.144
  328.5 2.9 copy.267
  331.5 3.1 copy.266
  334.6 0.7 reduce-scatter.13.cloned.1.call-update
  335.4 15.0 %reduce-scatter.31.cloned.1.call-done = f32[32,8,32]{2,1,0:T(8,128)} async-done(((f32[128,8,32]{2,1,0:T(8,128)}), f32[32,8,32]{2,1,0:T(8,128)}) %reduce-scatter.31.cloned.1.call-update) | async-done | bytes 32784 | tf_op jit(solution)/shard_map/reduce_scatter | solution.py:54
  350.4 23.5 %reduce-scatter.25.cloned.1.call-done = f32[32,8,32]{2,1,0:T(8,128)} async-done(((f32[128,8,32]{2,1,0:T(8,128)}), f32[32,8,32]{2,1,0:T(8,128)}) %reduce-scatter.25.cloned.1.call-update) | async-done | bytes 32784 | tf_op jit(solution)/shard_map/reduce_scatter | solution.py:54
  374.0 32.0 %reduce-scatter.13.cloned.1.call-done = f32[32,8,32]{1,0,2:T(8,128)} async-done(((f32[128,8,32]{1,0,2:T(8,128)}), f32[32,8,32]{1,0,2:T(8,128)}) %reduce-scatter.13.cloned.1.call-update) | async-done | bytes 32784 | tf_op jit(solution)/shard_map/reduce_scatter | solution.py:54
  406.1 1.9 copy.265
  408.2 20.8 %reduce-scatter.33.cloned.1.call-done = f32[8,8,32]{2,1,0:T(8,128)} async-done(((f32[32,8,32]{2,1,0:T(8,128)}), f32[8,8,32]{2,1,0:T(8,128)}) %reduce-scatter.33.cloned.1.call-update) | async-done | bytes 8208 | tf_op jit(solution)/shard_map/reduce_scatter | solution.py:54
  429.0 22.5 %reduce-scatter.27.cloned.1.call-done = f32[8,8,32]{2,1,0:T(8,128)} async-done(((f32[32,8,32]{2,1,0:T(8,128)}), f32[8,8,32]{2,1,0:T(8,128)}) %reduce-scatter.27.cloned.1.call-update) | async-done | bytes 8208 | tf_op jit(solution)/shard_map/reduce_scatter | solution.py:54
  454.1 9.8 %reduce-scatter.15.cloned.1.call-done = f32[16,8,32]{1,0,2:T(8,128)} async-done(((f32[32,8,32]{1,0,2:T(8,128)}), f32[16,8,32]{1,0,2:T(8,128)}) %reduce-scatter.15.cloned.1.call-update) | async-done | bytes 16400 | tf_op jit(solution)/shard_map/reduce_scatter | solution.py:54
  463.9 1.7 copy.264
  465.7 4.1 bitcast_select_fusion.1
  469.8 8.4 %reduce-scatter.19.cloned.1.call-done = f32[64,8,32]{2,1,0:T(8,128)} async-done(((f32[128,8,32]{2,1,0:T(8,128)}), f32[64,8,32]{2,1,0:T(8,128)}) %reduce-scatter.19.cloned.1.call-update) | async-done | bytes 65552 | tf_op jit(solution)/shard_map/reduce_scatter | solution.py:54
  478.3 13.6 %reduce-scatter.35.cloned.1.call-done = f32[4,8,32]{2,1,0:T(8,128)} async-done(((f32[8,8,32]{2,1,0:T(8,128)}), f32[4,8,32]{2,1,0:T(8,128)}) %reduce-scatter.35.cloned.1.call-update) | async-done | bytes 4112 | tf_op jit(solution)/shard_map/reduce_scatter | solution.py:54
  491.9 17.7 %all-reduce.3 = f32[4,8,32]{2,1,0:T(8,128)S(1)} all-reduce(f32[4,8,32]{2,1,0:T(8,128)} %reduce-scatter.35.cloned.1.call-done), channel_id=17, replica_groups=mesh['seq_0'=4,'seq_1'=2,'head_0'=4,'head_1'=4] {'head_0'}, use_global_device_ids=true, to_apply=%region_38.39.clone | all-reduce | flops 1024 | bytes 8192
  510.2 6.3 %reduce-scatter.29.cloned.1.call-done = f32[2,8,32]{2,1,0:T(8,128)} async-done(((f32[8,8,32]{2,1,0:T(8,128)}), f32[2,8,32]{2,1,0:T(8,128)}) %reduce-scatter.29.cloned.1.call-update) | async-done | bytes 2064 | tf_op jit(solution)/shard_map/reduce_scatter | solution.py:54
  516.5 2.6 all-reduce.2
  519.8 19.1 %reduce-scatter.17.cloned.1.call-done = f32[4,8,32]{2,1,0:T(8,128)} async-done(((f32[16,8,32]{2,1,0:T(8,128)}), f32[4,8,32]{2,1,0:T(8,128)}) %reduce-scatter.17.cloned.1.call-update) | async-done | bytes 4112 | tf_op jit(solution)/shard_map/reduce_scatter | solution.py:54
  538.8 17.5 %all-reduce = f32[4,8,32]{2,1,0:T(8,128)S(1)} all-reduce(f32[4,8,32]{2,1,0:T(8,128)} %reduce-scatter.17.cloned.1.call-done), channel_id=5, replica_groups=mesh['seq_0'=4,'seq_1'=2,'head_0'=4,'head_1'=4] {'head_1'}, use_global_device_ids=true, to_apply=%region_26.27.clone | all-reduce | flops 1024 | bytes 8192
  556.4 5.3 reduce-scatter.21.cloned.1.call-done
  562.3 22.0 %reduce-scatter.23.cloned.1.call-done = f32[4,8,32]{2,1,0:T(8,128)} async-done(((f32[16,8,32]{2,1,0:T(8,128)}), f32[4,8,32]{2,1,0:T(8,128)}) %reduce-scatter.23.cloned.1.call-update) | async-done | bytes 4112 | tf_op jit(solution)/shard_map/reduce_scatter | solution.py:54
  584.3 17.7 %all-reduce.1 = f32[4,8,32]{2,1,0:T(8,128)S(1)} all-reduce(f32[4,8,32]{2,1,0:T(8,128)} %reduce-scatter.23.cloned.1.call-done), channel_id=9, replica_groups=mesh['seq_0'=4,'seq_1'=2,'head_0'=4,'head_1'=4] {'seq_0'}, use_global_device_ids=true, to_apply=%region_30.31.clone | all-reduce | flops 1024 | bytes 8192
  602.7 0.7 copy.268
  (185 shorter events, 15.8 us)
Async XLA Ops:
  7.2 2.0 copy-start
  16.9 11.8 %copy-start.6 = (bf16[2,16,4096]{2,1,0:T(8,128)(2,1)S(1)}, bf16[2,16,4096]{2,1,0:T(8,128)(2,1)}, u32[]{:S(2)}) copy-start(bf16[2,16,4096]{2,1,0:T(8,128)(2,1)} %param.20) | copy-start | bytes 786436
  16.9 12.2 %copy-start.10 = (s32[1536]{0:T(1024)S(1)}, s32[1536]{0:T(1024)}, u32[]{:S(2)}) copy-start(s32[1536]{0:T(1024)} %param.18) | copy-start | bytes 18436
  16.9 12.2 %copy-start.12 = (s32[1536]{0:T(1024)S(1)}, s32[1536]{0:T(1024)}, u32[]{:S(2)}) copy-start(s32[1536]{0:T(1024)} %param.17) | copy-start | bytes 18436
  16.9 12.2 %copy-start.13 = (s32[1536]{0:T(1024)S(1)}, s32[1536]{0:T(1024)}, u32[]{:S(2)}) copy-start(s32[1536]{0:T(1024)} %param.16) | copy-start | bytes 18436
  16.9 14.2 %copy-start.9 = (s32[16]{0:T(128)S(1)}, s32[16]{0:T(128)}, u32[]{:S(2)}) copy-start(s32[16]{0:T(128)} %param.15) | copy-start | bytes 196
  16.9 62.8 %all-to-all-start = ((bf16[128,1,64,256]{3,2,1,0:T(8,128)(2,1)}), bf16[128,1,64,256]{3,2,1,0:T(8,128)(2,1)}, u32[]{:S(2)}, u32[]{:S(2)}) async-start(bf16[128,1,64,256]{3,2,1,0:T(8,128)(2,1)} %bitcast.483), calls=%async_computation | async-start | bytes 8388608 | tf_op jit(solution)/shard_map/all_to_all | solution.py:205
  28.6 91.2 %all-gather.5.cloned.1.call-start = ((), (), s32[]{:S(2)}) async-start(), calls=%async_computation.13 | async-start | bytes 2621440 | tf_op jit(solution)/shard_map/all_gather | solution.py:24
  82.7 1.7 copy-start.2
  82.7 3.3 copy-start.7
  84.3 1.7 copy-start.4
  91.7 45.0 %all-gather.7.cloned.1.call-start = ((), (), s32[]{:S(2)}) async-start(), calls=%async_computation.14 | async-start | bytes 1572864 | tf_op jit(solution)/shard_map/all_gather | solution.py:24
  122.7 49.7 %copy-start.11 = (bf16[2,16,32]{2,1,0:T(8,128)(2,1)S(1)}, bf16[2,16,32]{2,1,0:T(8,128)(2,1)}, u32[]{:S(2)}) copy-start(bf16[2,16,32]{2,1,0:T(8,128)(2,1)} %param.22) | copy-start | bytes 6148
  122.7 46.8 %all-gather.9.cloned.1.call-start = ((), (), s32[]{:S(2)}) async-start(), calls=%async_computation.15 | async-start | bytes 2621440 | tf_op jit(solution)/shard_map/all_gather | solution.py:24
  122.8 49.7 %copy-start.8 = (bf16[2,16,8,256]{3,2,1,0:T(8,128)(2,1)S(1)}, bf16[2,16,8,256]{3,2,1,0:T(8,128)(2,1)}, u32[]{:S(2)}) copy-start(bf16[2,16,8,256]{3,2,1,0:T(8,128)(2,1)} %param.21) | copy-start | bytes 393220
  139.1 36.1 %copy-start.16 = (bf16[32]{0:T(256)(128)(2,1)S(1)}, bf16[32]{0:T(256)(128)(2,1)}, u32[]{:S(2)}) copy-start(bf16[32]{0:T(256)(128)(2,1)} %param.24) | copy-start | bytes 196
  139.1 36.0 %copy-start.14 = (s32[2,16,2]{1,2,0:T(2,128)S(1)}, s32[2,16,2]{1,2,0:T(2,128)}, u32[]{:S(2)}) copy-start(s32[2,16,2]{1,2,0:T(2,128)} %param.26) | copy-start | bytes 772
  139.1 76.0 %all-gather.11.cloned.1.call-start = ((), (), s32[]{:S(2)}) async-start(), calls=%async_computation.16 | async-start | bytes 2621440 | tf_op jit(solution)/shard_map/all_gather | solution.py:24
  172.3 178.0 %reduce-scatter.31.cloned.1.call-start = ((), (), s32[]{:S(2)}) async-start(), calls=%async_computation.26 | async-start | bytes 655360 | tf_op jit(solution)/shard_map/reduce_scatter | solution.py:54
  216.9 1.6 copy-start.5
  218.5 3.6 copy-start.15
  331.4 74.7 %copy-start.3 = (f32[128,8,32]{1,0,2:T(8,128)S(1)}, f32[128,8,32]{1,0,2:T(8,128)}, u32[]{:S(2)}) copy-start(f32[128,8,32]{1,0,2:T(8,128)} %get-tuple-element.40) | copy-start | bytes 393220
  331.4 42.6 %reduce-scatter.25.cloned.1.call-start = ((), (), s32[]{:S(2)}) async-start(), calls=%async_computation.23 | async-start | bytes 655360 | tf_op jit(solution)/shard_map/reduce_scatter | solution.py:54
  334.5 117.1 %copy-start.20 = (u32[128]{0:T(128)S(1)}, u32[128]{0:T(128)}, u32[]{:S(2)}) copy-start(u32[128]{0:T(128)} %constant.244) | copy-start | bytes 1540
  334.6 117.7 %copy-start.19 = (u32[128]{0:T(128)S(1)}, u32[128]{0:T(128)}, u32[]{:S(2)}) copy-start(u32[128]{0:T(128)} %constant.240) | copy-start | bytes 1540
  334.6 118.3 %copy-start.18 = (u32[128]{0:T(128)S(1)}, u32[128]{0:T(128)}, u32[]{:S(2)}) copy-start(u32[128]{0:T(128)} %constant.236) | copy-start | bytes 1540
  334.6 118.9 %copy-start.17 = (u32[128]{0:T(128)S(1)}, u32[128]{0:T(128)}, u32[]{:S(2)}) copy-start(u32[128]{0:T(128)} %constant.232) | copy-start | bytes 1540
  334.6 71.5 %reduce-scatter.13.cloned.1.call-start = ((), (), s32[]{:S(2)}) async-start(), calls=%async_computation.17 | async-start | bytes 2621440 | tf_op jit(solution)/shard_map/reduce_scatter | solution.py:54
  335.3 93.6 %reduce-scatter.33.cloned.1.call-start = ((), (), s32[]{:S(2)}) async-start(), calls=%async_computation.27 | async-start | bytes 163840 | tf_op jit(solution)/shard_map/reduce_scatter | solution.py:54
  350.4 101.2 %reduce-scatter.27.cloned.1.call-start = ((), (), s32[]{:S(2)}) async-start(), calls=%async_computation.24 | async-start | bytes 163840 | tf_op jit(solution)/shard_map/reduce_scatter | solution.py:54
  374.0 89.9 %reduce-scatter.15.cloned.1.call-start = ((), (), s32[]{:S(2)}) async-start(), calls=%async_computation.18 | async-start | bytes 786432 | tf_op jit(solution)/shard_map/reduce_scatter | solution.py:54
  406.1 72.1 %reduce-scatter.19.cloned.1.call-start = ((), (), s32[]{:S(2)}) async-start(), calls=%async_computation.20 | async-start | bytes 786432 | tf_op jit(solution)/shard_map/reduce_scatter | solution.py:54
  408.1 83.8 %reduce-scatter.35.cloned.1.call-start = ((), (), s32[]{:S(2)}) async-start(), calls=%async_computation.28 | async-start | bytes 49152 | tf_op jit(solution)/shard_map/reduce_scatter | solution.py:54
  429.0 87.6 %reduce-scatter.29.cloned.1.call-start = ((), (), s32[]{:S(2)}) async-start(), calls=%async_computation.25 | async-start | bytes 40960 | tf_op jit(solution)/shard_map/reduce_scatter | solution.py:54
  451.6 87.3 %reduce-scatter.17.cloned.1.call-start = ((), (), s32[]{:S(2)}) async-start(), calls=%async_computation.19 | async-start | bytes 81920 | tf_op jit(solution)/shard_map/reduce_scatter | solution.py:54
  465.7 137.7 %copy-start.1 = (bf16[12,8,64,256]{3,2,1,0:T(8,128)(2,1)S(1)}, bf16[12,8,64,256]{3,2,1,0:T(8,128)(2,1)}, u32[]{:S(2)}) copy-start(bf16[12,8,64,256]{3,2,1,0:T(8,128)(2,1)} %param.19) | copy-start | bytes 9437188
  465.7 96.0 %reduce-scatter.21.cloned.1.call-start = ((), (), s32[]{:S(2)}) async-start(), calls=%async_computation.21 | async-start | bytes 327680 | tf_op jit(solution)/shard_map/reduce_scatter | solution.py:54
  478.2 106.0 %reduce-scatter.23.cloned.1.call-start = ((), (), s32[]{:S(2)}) async-start(), calls=%async_computation.22 | async-start | bytes 81920 | tf_op jit(solution)/shard_map/reduce_scatter | solution.py:54
Sparse Core Ops, SparseCore 0:
  91.8 27.9 all-gather.4
  122.8 11.3 all-gather.6
  139.2 30.1 all-gather.8
  172.5 31.3 all-gather.10
  331.5 18.7 reduce-scatter.30
  352.6 21.3 reduce-scatter.24
  376.4 29.6 reduce-scatter.12
  408.4 20.4 reduce-scatter.32
  431.3 20.1 reduce-scatter.26
  453.7 10.1 reduce-scatter.14
  466.3 11.8 reduce-scatter.18
  480.4 11.5 reduce-scatter.34
  494.3 22.2 reduce-scatter.28
  518.7 20.0 reduce-scatter.16
  541.1 20.5 reduce-scatter.20
  563.9 20.3 reduce-scatter.22
where the time goes:
time: 611 us; the launch traced here: 610 us
  waiting for transfers between devices  268 us (44%)
  blocking collectives  224 us (37%)
  local copies, waits for them, and re-layouts  42 us (7%)
  other arithmetic  29.7 us (5%)
  matrix products  18.5 us (3%)
  between operations  14.7 us (2%)
  starting transfers between devices  12.4 us (2%)
    reduce_scatter x12, waiting for transfers between devices, own_block(): blocks = lax.psum_scatter(blocks, axes[k], scatter_dimension=0, tiled=True)  198 us
    all_gather x8, blocking collectives, joined_all(): pieces = jax.tree.map(lambda part: lax.all_gather(part, axis), array)  76.6 us
    all_gather x1, blocking collectives, body(): features = lax.all_gather(normed, SEQ_HEAD, axis=1, tiled=True)  60 us
    unnamed x4, blocking collectives  55.5 us
    all_to_all x1, waiting for transfers between devices, body(): lax.all_to_all(packed.reshape(device_count, capacity, PAGE, 2 * HD), SEQ_...  38 us
    psum x4, blocking collectives, over_axes(): array = lax.psum(array, axis)  32.2 us
    all_gather x4, waiting for transfers between devices, joined_all(): pieces = jax.tree.map(lambda part: lax.all_gather(part, axis), array)  31.1 us
  transfers between devices with their start and end apart: 17, of which 15 were waited for; matrix products, arithmetic and copies ran while one was open for 6% of the time, Pallas kernels for 0%

commit v1 on v0

--- a/solution.py
+++ b/solution.py
@@ -272,7 +272,7 @@
     inverse_rms = lax.rsqrt(squares / D + EPSILON)
     logits = routed * inverse_rms[:, None]
     normed = (middle * inverse_rms[:, None] * gain_row).astype(jnp.bfloat16)
-    features = lax.all_gather(normed, SEQ_HEAD, axis=1, tiled=True)
+    features = jnp.concatenate(lax.all_gather(normed, SEQ_HEAD), axis=1)
     mixture = gate_mix(logits, routes.reshape(row_count, TOPK))
     local_experts = w_gate.shape[0]
     local_mix = lax.dynamic_slice_in_dim(mixture, seq_pos * local_experts, local_experts, axis=1)

time: 611 us -> 613 us (level)
  no operation moved by 1% of the time
where the time goes in v1:
time: 613 us; the launch traced here: 611 us
  waiting for transfers between devices  268 us (44%)
  blocking collectives  224 us (37%)
  local copies, waits for them, and re-layouts  43.6 us (7%)
  other arithmetic  29.7 us (5%)
  matrix products  18.5 us (3%)
  between operations  14.7 us (2%)
  starting transfers between devices  12.4 us (2%)
    reduce_scatter x12, waiting for transfers between devices, own_block(): blocks = lax.psum_scatter(blocks, axes[k], scatter_dimension=0, tiled=True)  198 us
    all_gather x8, blocking collectives, joined_all(): pieces = jax.tree.map(lambda part: lax.all_gather(part, axis), array)  76.6 us
    all_gather x1, blocking collectives, body(): features = jnp.concatenate(lax.all_gather(normed, SEQ_HEAD), axis=1)  60 us
    unnamed x4, blocking collectives  55.5 us
    all_to_all x1, waiting for transfers between devices, body(): lax.all_to_all(packed.reshape(device_count, capacity, PAGE, 2 * HD), SEQ_...  38 us
    psum x4, blocking collectives, over_axes(): array = lax.psum(array, axis)  32.2 us
    all_gather x4, waiting for transfers between devices, joined_all(): pieces = jax.tree.map(lambda part: lax.all_gather(part, axis), array)  31.1 us
  transfers between devices with their start and end apart: 17, of which 15 were waited for; matrix products, arithmetic and copies ran while one was open for 6% of the time, Pallas kernels for 0%

profile of v1, /device:TPU:0, one launch (start us, length us, event | category | flops | bytes accessed | tf_op | source)
XLA Modules:
  0.0 611.5 jit_solution(472810552915857388)
XLA Ops:
  7.2 0.9 broadcast_compare_fusion
  9.1 2.7 gather_fusion
  11.9 2.7 select_bitcast_fusion
  14.6 2.3 copy.241
  16.9 11.7 %all-to-all-start = ((bf16[128,1,64,256]{3,2,1,0:T(8,128)(2,1)}), bf16[128,1,64,256]{3,2,1,0:T(8,128)(2,1)}, u32[]{:S(2)}, u32[]{:S(2)}) async-start(bf16[128,1,64,256]{3,2,1,0:T(8,128)(2,1)} %bitcast.487), calls=%async_computation | async-start | bytes 8388608 | tf_op jit(solution)/shard_map/all_to_all | solution.py:205
  29.6 1.5 gather_fusion.2
  31.1 0.7 fusion.149
  31.8 9.8 %fusion.130 = (s32[96]{0:T(128)S(1)}, s32[96]{0:T(128)S(1)}) fusion(s32[]{:T(128)} %bitcast.17, s32[]{:T(128)} %bitcast.18, s32[]{:T(128)} %bitcast.19, s32[]{:T(128)} %bitcast.20, s32[]{:T(128)} %bitcast.21, s32[]{:T(128)} %bitcast.22, s32[]{:T(128)} %bitcast.23, s32[]{:T(128)} %bitcast.24, s32[]{:T(128)} %bitcast.25, s32[]{:T(128)} %bitcast.26, ...), kind=kLoop, calls=%fused_computation.273 | loop fusion | flops 4032 | bytes 1600 | tf_op jit(solution)/shard_map/jit(_take)/select_n | solution.py:116
  41.7 38.0 %all-to-all-done = bf16[128,1,64,256]{3,2,1,0:T(8,128)(2,1)} async-done(((bf16[128,1,64,256]{3,2,1,0:T(8,128)(2,1)}), bf16[128,1,64,256]{3,2,1,0:T(8,128)(2,1)}, u32[]{:S(2)}, u32[]{:S(2)}) %all-to-all-start) | async-done | bytes 4194336 | tf_op jit(solution)/shard_map/all_to_all | solution.py:205
  79.7 3.0 gather_fusion.1
  83.0 1.3 copy-done.2
  84.3 1.7 copy-done.4
  86.0 1.2 fusion.151
  87.5 0.7 gather_fusion.3
  88.4 2.0 fusion.8
  90.8 0.9 broadcast_select_fusion
  92.8 12.2 %all_gather.52 = f32[4,2,16,32]{3,2,1,0:T(8,128)S(1)} all-gather(f32[1,2,16,32]{3,2,1,0:T(8,128)S(1)} %copy.247), channel_id=1, replica_groups=mesh['seq_0'=4,'seq_1'=2,'head_0'=4,'head_1'=4] {'seq_0'}, dimensions={0}, use_global_device_ids=true | all-gather | bytes 20480 | tf_op jit(solution)/shard_map/all_gather | solution.py:24
  105.0 14.8 %all-gather.6.cloned.1.call-done = f32[4,2,16,32,128]{4,3,2,1,0:T(8,128)} async-done(((f32[1,2,16,32,128]{4,3,2,1,0:T(8,128)}), f32[4,2,16,32,128]{4,3,2,1,0:T(8,128)}) %all-gather.6.cloned.1.call-update) | async-done | bytes 2097168 | tf_op jit(solution)/shard_map/all_gather | solution.py:24
  119.8 2.9 fusion.45
  122.8 12.0 %all_gather.59 = f32[4,2,16,32]{3,2,1,0:T(8,128)S(1)} all-gather(f32[1,2,16,32]{3,2,1,0:T(8,128)S(1)} %copy.266), channel_id=1, replica_groups=mesh['seq_0'=4,'seq_1'=2,'head_0'=4,'head_1'=4] {'seq_0'}, dimensions={0}, use_global_device_ids=true | all-gather | bytes 20480 | tf_op jit(solution)/shard_map/all_gather | solution.py:24
  134.9 1.8 all_gather.54
  136.7 2.3 fusion.44
  139.2 1.8 all_gather.60
  141.0 12.1 %all_gather.56 = f32[4,2,16,32]{3,2,1,0:T(8,128)S(1)} all-gather(f32[1,2,16,32]{3,2,1,0:T(8,128)S(1)} %get-tuple-element.32), channel_id=1, replica_groups=mesh['seq_0'=4,'seq_1'=2,'head_0'=4,'head_1'=4] {'head_0'}, dimensions={0}, use_global_device_ids=true | all-gather | bytes 20480 | tf_op jit(solution)/shard_map/all_gather | solution.py:24
  153.1 16.3 %all-gather.10.cloned.1.call-done = f32[4,2,16,32,128]{4,3,2,1,0:T(8,128)} async-done(((f32[1,2,16,32,128]{4,3,2,1,0:T(8,128)}), f32[4,2,16,32,128]{4,3,2,1,0:T(8,128)}) %all-gather.10.cloned.1.call-update) | async-done | bytes 2097168 | tf_op jit(solution)/shard_map/all_gather | solution.py:24
  169.5 2.9 fusion.39
  172.5 2.4 fusion.152
  175.3 11.9 %all_gather.61 = f32[4,2,16,32]{3,2,1,0:T(8,128)S(1)} all-gather(f32[1,2,16,32]{3,2,1,0:T(8,128)S(1)} %get-tuple-element.31), channel_id=1, replica_groups=mesh['seq_0'=4,'seq_1'=2,'head_0'=4,'head_1'=4] {'head_0'}, dimensions={0}, use_global_device_ids=true | all-gather | bytes 20480 | tf_op jit(solution)/shard_map/all_gather | solution.py:24
  187.1 13.0 %all_gather.58 = f32[4,2,16,32]{3,2,1,0:T(8,128)S(1)} all-gather(f32[1,2,16,32]{3,2,1,0:T(8,128)S(1)} %get-tuple-element.30), channel_id=1, replica_groups=mesh['seq_0'=4,'seq_1'=2,'head_0'=4,'head_1'=4] {'head_1'}, dimensions={0}, use_global_device_ids=true | all-gather | bytes 20480 | tf_op jit(solution)/shard_map/all_gather | solution.py:24
  201.5 11.9 %all_gather.62 = f32[4,2,16,32]{3,2,1,0:T(8,128)S(1)} all-gather(f32[1,2,16,32]{3,2,1,0:T(8,128)S(1)} %get-tuple-element.29), channel_id=1, replica_groups=mesh['seq_0'=4,'seq_1'=2,'head_0'=4,'head_1'=4] {'head_1'}, dimensions={0}, use_global_device_ids=true | all-gather | bytes 20480 | tf_op jit(solution)/shard_map/all_gather | solution.py:24
  215.1 1.8 fusion.145
  218.5 3.6 multiply_reduce_fusion
  222.3 10.7 %all-reduce.6 = (f32[32]{0:T(128)S(1)}, f32[32,8]{0,1:T(8,128)S(1)}) all-reduce(f32[32]{0:T(128)S(1)} %get-tuple-element.95, f32[32,8]{0,1:T(8,128)S(1)} %fusion.112), channel_id=1, replica_groups=mesh['seq_0'=4,'seq_1'=2,'head_0'=4,'head_1'=4] {'seq_0'}, use_global_device_ids=true, to_apply=%region_17.18 | all-reduce | flops 288 | bytes 2304 | tf_op jit(solution)/shard_map/psum | solution.py:33
  233.0 2.5 all-reduce.7
  235.5 8.7 %all-reduce.5 = (f32[32]{0:T(128)S(1)}, f32[32,8]{0,1:T(8,128)S(1)}) all-reduce(f32[32]{0:T(128)S(1)} %get-tuple-element.15, f32[32,8]{0,1:T(8,128)S(1)} %get-tuple-element.16), channel_id=1, replica_groups=mesh['seq_0'=4,'seq_1'=2,'head_0'=4,'head_1'=4] {'head_0'}, use_global_device_ids=true, to_apply=%region_19.20 | all-reduce | flops 288 | bytes 2304 | tf_op jit(solution)/shard_map/psum | solution.py:33
  244.3 10.3 %all-reduce.4 = (f32[32]{0:T(128)S(1)}, f32[32,8]{0,1:T(8,128)S(1)}) all-reduce(f32[32]{0:T(128)S(1)} %get-tuple-element.11, f32[32,8]{0,1:T(8,128)S(1)} %get-tuple-element.12), channel_id=1, replica_groups=mesh['seq_0'=4,'seq_1'=2,'head_0'=4,'head_1'=4] {'head_1'}, use_global_device_ids=true, to_apply=%region_20.21 | all-reduce | flops 288 | bytes 2304 | tf_op jit(solution)/shard_map/psum | solution.py:33
  254.7 60.0 %all-gather = bf16[4096,32]{1,0:T(8,128)(2,1)S(1)} all-gather(bf16[32,32]{1,0:T(8,128)(2,1)S(1)} %copy.275), channel_id=2, replica_groups=mesh['seq_0'=4,'seq_1'=2,'head_0'=4,'head_1'=4] {'seq_0','seq_1','head_0..., dimensions={0}, use_global_device_ids=true | all-gather | bytes 264192 | tf_op jit(solution)/shard_map/all_gather | solution.py:275
  315.1 1.1 reshape.808
  316.3 3.0 fusion.14
  319.3 5.1 fusion
  324.4 0.7 reshape.813
  325.1 4.9 fusion.144
  330.0 2.9 copy.281
  333.0 3.1 copy.280
  336.2 0.7 reduce-scatter.13.cloned.1.call-update
  337.0 15.0 %reduce-scatter.31.cloned.1.call-done = f32[32,8,32]{2,1,0:T(8,128)} async-done(((f32[128,8,32]{2,1,0:T(8,128)}), f32[32,8,32]{2,1,0:T(8,128)}) %reduce-scatter.31.cloned.1.call-update) | async-done | bytes 32784 | tf_op jit(solution)/shard_map/reduce_scatter | solution.py:54
  352.0 23.5 %reduce-scatter.25.cloned.1.call-done = f32[32,8,32]{2,1,0:T(8,128)} async-done(((f32[128,8,32]{2,1,0:T(8,128)}), f32[32,8,32]{2,1,0:T(8,128)}) %reduce-scatter.25.cloned.1.call-update) | async-done | bytes 32784 | tf_op jit(solution)/shard_map/reduce_scatter | solution.py:54
  375.6 32.0 %reduce-scatter.13.cloned.1.call-done = f32[32,8,32]{1,0,2:T(8,128)} async-done(((f32[128,8,32]{1,0,2:T(8,128)}), f32[32,8,32]{1,0,2:T(8,128)}) %reduce-scatter.13.cloned.1.call-update) | async-done | bytes 32784 | tf_op jit(solution)/shard_map/reduce_scatter | solution.py:54
  407.7 1.9 copy.279
  409.7 20.8 %reduce-scatter.33.cloned.1.call-done = f32[8,8,32]{2,1,0:T(8,128)} async-done(((f32[32,8,32]{2,1,0:T(8,128)}), f32[8,8,32]{2,1,0:T(8,128)}) %reduce-scatter.33.cloned.1.call-update) | async-done | bytes 8208 | tf_op jit(solution)/shard_map/reduce_scatter | solution.py:54
  430.6 22.5 %reduce-scatter.27.cloned.1.call-done = f32[8,8,32]{2,1,0:T(8,128)} async-done(((f32[32,8,32]{2,1,0:T(8,128)}), f32[8,8,32]{2,1,0:T(8,128)}) %reduce-scatter.27.cloned.1.call-update) | async-done | bytes 8208 | tf_op jit(solution)/shard_map/reduce_scatter | solution.py:54
  455.7 9.8 %reduce-scatter.15.cloned.1.call-done = f32[16,8,32]{1,0,2:T(8,128)} async-done(((f32[32,8,32]{1,0,2:T(8,128)}), f32[16,8,32]{1,0,2:T(8,128)}) %reduce-scatter.15.cloned.1.call-update) | async-done | bytes 16400 | tf_op jit(solution)/shard_map/reduce_scatter | solution.py:54
  465.5 1.7 copy.278
  467.3 4.1 bitcast_select_fusion.1
  471.4 8.4 %reduce-scatter.19.cloned.1.call-done = f32[64,8,32]{2,1,0:T(8,128)} async-done(((f32[128,8,32]{2,1,0:T(8,128)}), f32[64,8,32]{2,1,0:T(8,128)}) %reduce-scatter.19.cloned.1.call-update) | async-done | bytes 65552 | tf_op jit(solution)/shard_map/reduce_scatter | solution.py:54
  479.9 13.6 %reduce-scatter.35.cloned.1.call-done = f32[4,8,32]{2,1,0:T(8,128)} async-done(((f32[8,8,32]{2,1,0:T(8,128)}), f32[4,8,32]{2,1,0:T(8,128)}) %reduce-scatter.35.cloned.1.call-update) | async-done | bytes 4112 | tf_op jit(solution)/shard_map/reduce_scatter | solution.py:54
  493.5 17.7 %all-reduce.3 = f32[4,8,32]{2,1,0:T(8,128)S(1)} all-reduce(f32[4,8,32]{2,1,0:T(8,128)} %reduce-scatter.35.cloned.1.call-done), channel_id=18, replica_groups=mesh['seq_0'=4,'seq_1'=2,'head_0'=4,'head_1'=4] {'head_0'}, use_global_device_ids=true, to_apply=%region_38.39.clone | all-reduce | flops 1024 | bytes 8192
  511.8 6.3 %reduce-scatter.29.cloned.1.call-done = f32[2,8,32]{2,1,0:T(8,128)} async-done(((f32[8,8,32]{2,1,0:T(8,128)}), f32[2,8,32]{2,1,0:T(8,128)}) %reduce-scatter.29.cloned.1.call-update) | async-done | bytes 2064 | tf_op jit(solution)/shard_map/reduce_scatter | solution.py:54
  518.1 2.6 all-reduce.2
  521.4 19.1 %reduce-scatter.17.cloned.1.call-done = f32[4,8,32]{2,1,0:T(8,128)} async-done(((f32[16,8,32]{2,1,0:T(8,128)}), f32[4,8,32]{2,1,0:T(8,128)}) %reduce-scatter.17.cloned.1.call-update) | async-done | bytes 4112 | tf_op jit(solution)/shard_map/reduce_scatter | solution.py:54
  540.4 17.5 %all-reduce = f32[4,8,32]{2,1,0:T(8,128)S(1)} all-reduce(f32[4,8,32]{2,1,0:T(8,128)} %reduce-scatter.17.cloned.1.call-done), channel_id=6, replica_groups=mesh['seq_0'=4,'seq_1'=2,'head_0'=4,'head_1'=4] {'head_1'}, use_global_device_ids=true, to_apply=%region_26.27.clone | all-reduce | flops 1024 | bytes 8192
  558.0 5.3 reduce-scatter.21.cloned.1.call-done
  563.9 22.0 %reduce-scatter.23.cloned.1.call-done = f32[4,8,32]{2,1,0:T(8,128)} async-done(((f32[16,8,32]{2,1,0:T(8,128)}), f32[4,8,32]{2,1,0:T(8,128)}) %reduce-scatter.23.cloned.1.call-update) | async-done | bytes 4112 | tf_op jit(solution)/shard_map/reduce_scatter | solution.py:54
  585.8 17.7 %all-reduce.1 = f32[4,8,32]{2,1,0:T(8,128)S(1)} all-reduce(f32[4,8,32]{2,1,0:T(8,128)} %reduce-scatter.23.cloned.1.call-done), channel_id=10, replica_groups=mesh['seq_0'=4,'seq_1'=2,'head_0'=4,'head_1'=4] {'seq_0'}, use_global_device_ids=true, to_apply=%region_30.31.clone | all-reduce | flops 1024 | bytes 8192
  (188 shorter events, 17.0 us)
Async XLA Ops:
  7.2 2.0 copy-start
  16.9 11.8 %copy-start.6 = (bf16[2,16,4096]{2,1,0:T(8,128)(2,1)S(1)}, bf16[2,16,4096]{2,1,0:T(8,128)(2,1)}, u32[]{:S(2)}) copy-start(bf16[2,16,4096]{2,1,0:T(8,128)(2,1)} %param.20) | copy-start | bytes 786436
  16.9 12.2 %copy-start.10 = (s32[1536]{0:T(1024)S(1)}, s32[1536]{0:T(1024)}, u32[]{:S(2)}) copy-start(s32[1536]{0:T(1024)} %param.18) | copy-start | bytes 18436
  16.9 12.2 %copy-start.12 = (s32[1536]{0:T(1024)S(1)}, s32[1536]{0:T(1024)}, u32[]{:S(2)}) copy-start(s32[1536]{0:T(1024)} %param.17) | copy-start | bytes 18436
  16.9 12.2 %copy-start.13 = (s32[1536]{0:T(1024)S(1)}, s32[1536]{0:T(1024)}, u32[]{:S(2)}) copy-start(s32[1536]{0:T(1024)} %param.16) | copy-start | bytes 18436
  16.9 14.2 %copy-start.9 = (s32[16]{0:T(128)S(1)}, s32[16]{0:T(128)}, u32[]{:S(2)}) copy-start(s32[16]{0:T(128)} %param.15) | copy-start | bytes 196
  16.9 62.8 %all-to-all-start = ((bf16[128,1,64,256]{3,2,1,0:T(8,128)(2,1)}), bf16[128,1,64,256]{3,2,1,0:T(8,128)(2,1)}, u32[]{:S(2)}, u32[]{:S(2)}) async-start(bf16[128,1,64,256]{3,2,1,0:T(8,128)(2,1)} %bitcast.487), calls=%async_computation | async-start | bytes 8388608 | tf_op jit(solution)/shard_map/all_to_all | solution.py:205
  28.6 91.2 %all-gather.6.cloned.1.call-start = ((), (), s32[]{:S(2)}) async-start(), calls=%async_computation.13 | async-start | bytes 2621440 | tf_op jit(solution)/shard_map/all_gather | solution.py:24
  82.7 1.7 copy-start.2
  82.7 3.3 copy-start.7
  84.3 1.7 copy-start.4
  91.7 45.0 %all-gather.8.cloned.1.call-start = ((), (), s32[]{:S(2)}) async-start(), calls=%async_computation.14 | async-start | bytes 1572864 | tf_op jit(solution)/shard_map/all_gather | solution.py:24
  122.7 49.7 %copy-start.11 = (bf16[2,16,32]{2,1,0:T(8,128)(2,1)S(1)}, bf16[2,16,32]{2,1,0:T(8,128)(2,1)}, u32[]{:S(2)}) copy-start(bf16[2,16,32]{2,1,0:T(8,128)(2,1)} %param.22) | copy-start | bytes 6148
  122.7 46.8 %all-gather.10.cloned.1.call-start = ((), (), s32[]{:S(2)}) async-start(), calls=%async_computation.15 | async-start | bytes 2621440 | tf_op jit(solution)/shard_map/all_gather | solution.py:24
  122.8 49.7 %copy-start.8 = (bf16[2,16,8,256]{3,2,1,0:T(8,128)(2,1)S(1)}, bf16[2,16,8,256]{3,2,1,0:T(8,128)(2,1)}, u32[]{:S(2)}) copy-start(bf16[2,16,8,256]{3,2,1,0:T(8,128)(2,1)} %param.21) | copy-start | bytes 393220
  139.1 36.1 %copy-start.16 = (bf16[32]{0:T(256)(128)(2,1)S(1)}, bf16[32]{0:T(256)(128)(2,1)}, u32[]{:S(2)}) copy-start(bf16[32]{0:T(256)(128)(2,1)} %param.24) | copy-start | bytes 196
  139.1 36.0 %copy-start.14 = (s32[2,16,2]{1,2,0:T(2,128)S(1)}, s32[2,16,2]{1,2,0:T(2,128)}, u32[]{:S(2)}) copy-start(s32[2,16,2]{1,2,0:T(2,128)} %param.26) | copy-start | bytes 772
  139.1 76.0 %all-gather.12.cloned.1.call-start = ((), (), s32[]{:S(2)}) async-start(), calls=%async_computation.16 | async-start | bytes 2621440 | tf_op jit(solution)/shard_map/all_gather | solution.py:24
  172.3 179.6 %reduce-scatter.31.cloned.1.call-start = ((), (), s32[]{:S(2)}) async-start(), calls=%async_computation.26 | async-start | bytes 655360 | tf_op jit(solution)/shard_map/reduce_scatter | solution.py:54
  216.9 1.6 copy-start.5
  218.5 3.6 copy-start.15
  333.0 74.7 %copy-start.3 = (f32[128,8,32]{1,0,2:T(8,128)S(1)}, f32[128,8,32]{1,0,2:T(8,128)}, u32[]{:S(2)}) copy-start(f32[128,8,32]{1,0,2:T(8,128)} %get-tuple-element.40) | copy-start | bytes 393220
  333.0 42.6 %reduce-scatter.25.cloned.1.call-start = ((), (), s32[]{:S(2)}) async-start(), calls=%async_computation.23 | async-start | bytes 655360 | tf_op jit(solution)/shard_map/reduce_scatter | solution.py:54
  336.1 117.1 %copy-start.20 = (u32[128]{0:T(128)S(1)}, u32[128]{0:T(128)}, u32[]{:S(2)}) copy-start(u32[128]{0:T(128)} %constant.244) | copy-start | bytes 1540
  336.1 117.7 %copy-start.19 = (u32[128]{0:T(128)S(1)}, u32[128]{0:T(128)}, u32[]{:S(2)}) copy-start(u32[128]{0:T(128)} %constant.240) | copy-start | bytes 1540
  336.1 118.3 %copy-start.18 = (u32[128]{0:T(128)S(1)}, u32[128]{0:T(128)}, u32[]{:S(2)}) copy-start(u32[128]{0:T(128)} %constant.236) | copy-start | bytes 1540
  336.2 118.9 %copy-start.17 = (u32[128]{0:T(128)S(1)}, u32[128]{0:T(128)}, u32[]{:S(2)}) copy-start(u32[128]{0:T(128)} %constant.232) | copy-start | bytes 1540
  336.2 71.5 %reduce-scatter.13.cloned.1.call-start = ((), (), s32[]{:S(2)}) async-start(), calls=%async_computation.17 | async-start | bytes 2621440 | tf_op jit(solution)/shard_map/reduce_scatter | solution.py:54
  336.9 93.6 %reduce-scatter.33.cloned.1.call-start = ((), (), s32[]{:S(2)}) async-start(), calls=%async_computation.27 | async-start | bytes 163840 | tf_op jit(solution)/shard_map/reduce_scatter | solution.py:54
  352.0 101.1 %reduce-scatter.27.cloned.1.call-start = ((), (), s32[]{:S(2)}) async-start(), calls=%async_computation.24 | async-start | bytes 163840 | tf_op jit(solution)/shard_map/reduce_scatter | solution.py:54
  375.6 89.9 %reduce-scatter.15.cloned.1.call-start = ((), (), s32[]{:S(2)}) async-start(), calls=%async_computation.18 | async-start | bytes 786432 | tf_op jit(solution)/shard_map/reduce_scatter | solution.py:54
  407.7 72.1 %reduce-scatter.19.cloned.1.call-start = ((), (), s32[]{:S(2)}) async-start(), calls=%async_computation.20 | async-start | bytes 786432 | tf_op jit(solution)/shard_map/reduce_scatter | solution.py:54
  409.7 83.8 %reduce-scatter.35.cloned.1.call-start = ((), (), s32[]{:S(2)}) async-start(), calls=%async_computation.28 | async-start | bytes 49152 | tf_op jit(solution)/shard_map/reduce_scatter | solution.py:54
  430.5 87.6 %reduce-scatter.29.cloned.1.call-start = ((), (), s32[]{:S(2)}) async-start(), calls=%async_computation.25 | async-start | bytes 40960 | tf_op jit(solution)/shard_map/reduce_scatter | solution.py:54
  453.1 87.3 %reduce-scatter.17.cloned.1.call-start = ((), (), s32[]{:S(2)}) async-start(), calls=%async_computation.19 | async-start | bytes 81920 | tf_op jit(solution)/shard_map/reduce_scatter | solution.py:54
  467.2 137.7 %copy-start.1 = (bf16[12,8,64,256]{3,2,1,0:T(8,128)(2,1)S(1)}, bf16[12,8,64,256]{3,2,1,0:T(8,128)(2,1)}, u32[]{:S(2)}) copy-start(bf16[12,8,64,256]{3,2,1,0:T(8,128)(2,1)} %param.19) | copy-start | bytes 9437188
  467.3 96.0 %reduce-scatter.21.cloned.1.call-start = ((), (), s32[]{:S(2)}) async-start(), calls=%async_computation.21 | async-start | bytes 327680 | tf_op jit(solution)/shard_map/reduce_scatter | solution.py:54
  479.8 106.0 %reduce-scatter.23.cloned.1.call-start = ((), (), s32[]{:S(2)}) async-start(), calls=%async_computation.22 | async-start | bytes 81920 | tf_op jit(solution)/shard_map/reduce_scatter | solution.py:54
Sparse Core Ops, SparseCore 0:
  91.8 27.9 all-gather.5
  122.8 11.3 all-gather.7
  139.2 30.1 all-gather.9
  172.5 31.3 all-gather.11
  333.1 18.8 reduce-scatter.30
  354.2 21.3 reduce-scatter.24
  378.0 29.6 reduce-scatter.12
  410.0 20.4 reduce-scatter.32
  432.9 20.1 reduce-scatter.26
  455.3 10.1 reduce-scatter.14
  467.9 11.8 reduce-scatter.18
  481.9 11.5 reduce-scatter.34
  495.9 22.2 reduce-scatter.28
  520.3 20.0 reduce-scatter.16
  542.6 20.5 reduce-scatter.20
  565.5 20.3 reduce-scatter.22
